TPU v7x, 32 devices: a whole 2x2x4 slice. The times are simulated.
32 devices in a mesh: ma: 4 (over x, core), ell: 8 (over z, y).
Axes of the slice: x: 2, y: 2, z: 4, core: 2. Of those that a mesh axis runs over, the one named last changes fastest.
Arguments:
- legendre: bfloat16 [3, 2048, 2, 4096], P(None, 'ma', None, 'ell'), may hold values from -6 to 6
- harmonics: bfloat16 [2048, 3, 2, 4, 4096], P('ma', None, None, None, 'ell'), may hold values from -0.0014648438 to 0.0014648438
- slot_orders: int32 [2048], replicated, may hold values from 0 to 2047, each once
- cycle_index: int32 [2], replicated, may hold values from 2048 to 4095
Outputs:
- maps: float32 [4, 3, 4, 8192], P('ma', None, None, 'ell')
Inputs may be any that keep to these rules, and one draw needn't show every extreme that they name: `slot_orders`: every number from 0 to 2047 appears once.
All inputs are finite; a program needn't handle non-finite values.
Results may differ from a plain program's by a relative error of at most 0.0003.
Values sent between devices are 32-bit elements; how exact they have to be, the bound alone decides.
A program may use at most 128 MiB of HBM per device.

v0:
```python
import functools
import math

import jax
import jax.numpy as jnp
import numpy as np
from jax import lax
from jax.experimental import pallas as pl
from jax.experimental.pallas import tpu as pltpu
from jax.sharding import PartitionSpec as P


def column_weights(lower_order, first_column, columns_count, full_width):
    columns = first_column + jnp.arange(columns_count, dtype=jnp.int32)
    boundary = (full_width - 1 - lower_order)[:, None]
    lower_part = (columns[None, :] < boundary).astype(jnp.float32)
    upper_part = ((columns[None, :] >= boundary) & (columns[None, :] < full_width - 1)).astype(
        jnp.float32
    )
    lower_sign = (1 - 2 * (columns[None, :] % 2)).astype(jnp.float32)
    upper_sign = (1 - 2 * ((columns[None, :] + 1 + lower_order[:, None]) % 2)).astype(jnp.float32)
    return jnp.stack(
        [lower_part, lower_part * lower_sign, upper_part, upper_part * upper_sign], axis=1
    )


def spin_fields(plain, plus, minus):
    hemisphere = jnp.array([1.0, -1.0], jnp.float32).reshape(1, 1, 1, 2, 1, 1, 1)
    minus = minus * hemisphere
    temp_real = plain[:, :, :, :, 0]
    temp_imag = plain[:, :, :, :, 1]
    eplus_real = plus[:, :, :, :, 0, 0]
    eplus_imag = plus[:, :, :, :, 0, 1]
    bplus_real = plus[:, :, :, :, 1, 0]
    bplus_imag = plus[:, :, :, :, 1, 1]
    eminus_real = minus[:, :, :, :, 0, 0]
    eminus_imag = minus[:, :, :, :, 0, 1]
    bminus_real = minus[:, :, :, :, 1, 0]
    bminus_imag = minus[:, :, :, :, 1, 1]
    stokes_q_real = -(eplus_real - bminus_imag)
    stokes_q_imag = -(eplus_imag + bminus_real)
    stokes_u_real = -(bplus_real + eminus_imag)
    stokes_u_imag = -(bplus_imag - eminus_real)
    return jnp.stack(
        [
            jnp.stack([temp_real, temp_imag]),
            jnp.stack([stokes_q_real, stokes_q_imag]),
            jnp.stack([stokes_u_real, stokes_u_imag]),
        ]
    )


def place_orders(cycle_orders, lower_all):
    highest = lax.Precision.HIGHEST
    half = lower_all.shape[0]
    width = min(512, half)
    pieces = []
    for start in range(0, half, width):
        targets = start + jnp.arange(width, dtype=jnp.int32)
        onehot = (lower_all[:, None] == targets[None, :]).astype(jnp.float32)
        pieces.append(jnp.einsum("abcdes,sm->abcdem", cycle_orders, onehot, precision=highest))
    placed = jnp.concatenate(pieces, axis=-1)
    return jnp.concatenate([placed[..., 0, :], jnp.flip(placed[..., 1, :], axis=-1)], axis=-1)


def cycle_synthesis(coeff, shift, first_group, group_count):
    highest = lax.Precision.HIGHEST
    cycles_count = coeff.shape[0]
    components = coeff.shape[3]
    orders_count = coeff.shape[-1]
    pixels = 2 * orders_count
    outer = pixels // 128
    groups = orders_count // 128
    orders = jnp.arange(orders_count, dtype=jnp.int32)
    phase = (orders[None, :] * shift[:, None] % (2 * pixels)).astype(jnp.float32) * (
        math.pi / pixels
    )
    factor = jnp.where(orders == 0, 1.0, 2.0).astype(jnp.float32)
    cosine = (jnp.cos(phase) * factor)[:, None, None, :]
    sine = (jnp.sin(phase) * factor)[:, None, None, :]
    real_part = coeff[:, :, 0]
    imag_part = coeff[:, :, 1]
    shifted_real = (real_part * cosine - imag_part * sine).reshape(
        cycles_count, 3, components, groups, 128
    )
    shifted_imag = (real_part * sine + imag_part * cosine).reshape(
        cycles_count, 3, components, groups, 128
    )
    group_ids = jnp.arange(groups, dtype=jnp.int32)
    outer_ids = jnp.arange(outer, dtype=jnp.int32)
    inner_ids = jnp.arange(128, dtype=jnp.int32)
    angle_one = (group_ids[:, None] * outer_ids[None, :] % outer).astype(jnp.float32) * (
        2.0 * math.pi / outer
    )
    cos_one = jnp.cos(angle_one)
    sin_one = jnp.sin(angle_one)
    first_real = jnp.einsum(
        "xyzab,ak->xyzkb", shifted_real, cos_one, precision=highest
    ) - jnp.einsum("xyzab,ak->xyzkb", shifted_imag, sin_one, precision=highest)
    first_imag = jnp.einsum(
        "xyzab,ak->xyzkb", shifted_real, sin_one, precision=highest
    ) + jnp.einsum("xyzab,ak->xyzkb", shifted_imag, cos_one, precision=highest)
    angle_two = (outer_ids[:, None] * inner_ids[None, :] % pixels).astype(jnp.float32) * (
        2.0 * math.pi / pixels
    )
    cos_two = jnp.cos(angle_two)
    sin_two = jnp.sin(angle_two)
    twist_real = first_real * cos_two - first_imag * sin_two
    twist_imag = first_real * sin_two + first_imag * cos_two
    local_ids = first_group + jnp.arange(group_count, dtype=jnp.int32)
    angle_three = (inner_ids[:, None] * local_ids[None, :] % 128).astype(jnp.float32) * (
        2.0 * math.pi / 128
    )
    cos_three = jnp.cos(angle_three)
    sin_three = jnp.sin(angle_three)
    result = jnp.einsum("xyzkb,bq->xyzqk", twist_real, cos_three, precision=highest) - jnp.einsum(
        "xyzkb,bq->xyzqk", twist_imag, sin_three, precision=highest
    )
    return result.reshape(cycles_count, 3, components, group_count * outer)


def general_body(legendre, harmonics, slot_orders, cycle_index):
    ell_count = lax.axis_size("ell")
    slots_here = harmonics.shape[0]
    columns_here = harmonics.shape[-1]
    components = harmonics.shape[3]
    full_width = 2 * slot_orders.shape[0]
    pairs = cycle_index.shape[0]
    lower_here = lax.dynamic_slice_in_dim(
        slot_orders, lax.axis_index("ma") * slots_here, slots_here
    )
    weights = column_weights(
        lower_here, lax.axis_index("ell") * columns_here, columns_here, full_width
    ).astype(jnp.bfloat16)
    packed = harmonics[:, None] * weights[:, :, None, None, None, :]
    plain = jnp.einsum(
        "srj,sqpcj->srqpc", legendre[0], packed[:, :, 0], preferred_element_type=jnp.float32
    )
    plus = jnp.einsum(
        "srj,sqkpcj->srqkpc", legendre[1], packed[:, :, 1:3], preferred_element_type=jnp.float32
    )
    minus = jnp.einsum(
        "srj,sqkpcj->srqkpc", legendre[2], packed[:, :, 1:3], preferred_element_type=jnp.float32
    )
    plain = plain.reshape(slots_here, pairs, 2, 2, 2, components)
    plus = plus.reshape(slots_here, pairs, 2, 2, 2, 2, components)
    minus = minus.reshape(slots_here, pairs, 2, 2, 2, 2, components)
    fields = spin_fields(plain, plus, minus)
    cycle_sums = fields.transpose(5, 3, 0, 1, 6, 4, 2).reshape(
        2 * pairs, 3, 2, components, 2, slots_here
    )
    summed = lax.psum(cycle_sums, "ell")
    cycle_orders = lax.all_to_all(summed, "ma", split_axis=0, concat_axis=5, tiled=True)
    slot_ids = jnp.arange(slot_orders.shape[0], dtype=jnp.int32)
    lower_all = slot_orders[slot_ids]
    coeff = place_orders(cycle_orders, lower_all)
    cycles_here = cycle_orders.shape[0]
    cycle_ids = lax.axis_index("ma") * cycles_here + jnp.arange(cycles_here, dtype=jnp.int32)
    shift = cycle_index[cycle_ids % pairs] % 2
    per_device = 128 // ell_count
    return cycle_synthesis(coeff, shift, lax.axis_index("ell") * per_device, per_device)


LANES = 128
NT = (((1,), (1,)), ((), ()))
SUB = 32


def rotate_sums(group, lane_pair, sub_pair):
    turned = None
    for step in range(4):
        mixed = group[step]
        for pair in range(1, 4):
            mixed = jnp.where(sub_pair == pair, group[(pair + step) % 4], mixed)
        if step == 0:
            turned = mixed
        else:
            mixed = pltpu.roll(mixed, 2 * step, 0)
            turned = jnp.where((sub_pair - lane_pair) % 4 == step, mixed, turned)
    return turned


def fused_kernel(
    width, slots, columns,
    cycle_hbm, orders_hbm, order_rows_hbm, tables_hbm, packed_hbm,
    phase_hbm, first_hbm, twist_hbm, last_hbm, out_ref,
    cycle_ref, orders_ref, rows_ref, table_ref, even_ref, plain_ref,
    phase_ref, first_ref, twist_ref, last_ref,
    spin_part, plain_part, send_ref, held_ref, left_ref, right_ref, pixel_ref, landed_ref,
    small_sem, spin_sem, plain_sem, send_sem, recv_sem, pixel_send, pixel_recv,
):
    highest = lax.Precision.HIGHEST
    owners, sources = lax.axis_size("ma"), lax.axis_size("ell")
    my_owner, my_source = lax.axis_index("ma"), lax.axis_index("ell")
    me = my_owner * sources + my_source
    mesh_ids = pl.DeviceIdType.MESH
    count = owners * sources
    quads = slots // 4
    half = quads // 2
    subs = quads // SUB
    plain_subs = half // SUB

    small = [
        pltpu.make_async_copy(a, b, small_sem.at[i])
        for i, (a, b) in enumerate(
            [
                (orders_hbm, orders_ref),
                (order_rows_hbm, rows_ref),
                (cycle_hbm, cycle_ref),
                (phase_hbm, phase_ref),
                (first_hbm, first_ref),
                (twist_hbm, twist_ref),
                (last_hbm, last_ref),
            ]
        )
    ]

    def spin_copies(sub):
        here = pl.ds(sub * SUB, SUB)
        copies = []
        for g in range(4):
            copies.append((tables_hbm.at[pl.ds(1, 2), g, here], table_ref.at[pl.ds(1, 2), here, :, g]))
            for k in range(2):
                copies.append((packed_hbm.at[g, here, pl.ds(2, 4), k], even_ref.at[here, k, g]))
        return [
            pltpu.make_async_copy(a, b, spin_sem.at[sub, i]) for i, (a, b) in enumerate(copies)
        ]

    def plain_copies(sub):
        copies = []
        to = pl.ds(sub * SUB, SUB)
        for ab in range(2):
            here = pl.ds(ab * half + sub * SUB, SUB)
            for g in range(4):
                copies.append((tables_hbm.at[0, g, here], table_ref.at[0, here, :, g]))
                for k in range(2):
                    copies.append((packed_hbm.at[g, here, pl.ds(0, 2), k], plain_ref.at[to, k, ab, g]))
        return [
            pltpu.make_async_copy(a, b, plain_sem.at[sub, i]) for i, (a, b) in enumerate(copies)
        ]

    small[0].start()
    small[1].start()

    def start_spin(sub, carry):
        for copy in spin_copies(sub):
            copy.start()
        return carry

    def start_plain(sub, carry):
        for copy in plain_copies(sub):
            copy.start()
        return carry

    lax.fori_loop(0, subs, start_spin, 0)
    lax.fori_loop(0, plain_subs, start_plain, 0)
    for copy in small[2:]:
        copy.start()

    def shifted_device(step):
        owner = lax.rem(my_owner + step // sources, owners)
        source = lax.rem(my_source + step % sources, sources)
        return owner, source

    barrier = pltpu.get_barrier_semaphore()

    def greet(step, carry):
        pl.semaphore_signal(
            barrier, inc=1, device_id=shifted_device(step), device_id_type=mesh_ids
        )
        return carry

    lax.fori_loop(1, count, greet, 0)

    lane8 = lax.broadcasted_iota(jnp.int32, (8, LANES), 1)
    sub8 = lax.broadcasted_iota(jnp.int32, (8, LANES), 0)
    lane_low = lax.broadcasted_iota(jnp.int32, (4, LANES), 1) < 64
    small[0].wait()
    small[1].wait()

    def ordered_rows(owner):
        lower = rows_ref[owner]
        turned = pltpu.roll(lower, 64, 1)
        return jnp.concatenate(
            [
                jnp.where(lane_low, lower, width - 1 - turned),
                jnp.where(lane_low, turned, width - 1 - lower),
            ],
            axis=0,
        )

    lane_rows = lax.broadcasted_iota(jnp.int32, (LANES, LANES), 0)
    for near in range(owners):
        ordered = ordered_rows(lax.rem(my_owner + owners - near, owners))
        for k in range(8):
            at = ((k // 4) * owners + near) * 4 + k % 4
            right_ref[:, at * LANES : (at + 1) * LANES] = jnp.where(
                lane_rows == ordered[k : k + 1, :] % LANES, 1.0, 0.0
            ).astype(jnp.bfloat16)

    first_column = my_source * columns
    lane16 = lax.broadcasted_iota(jnp.int32, (16, LANES), 1)
    sub16 = lax.broadcasted_iota(jnp.int32, (16, LANES), 0)
    alternate = (1 - 2 * (lane16 % 2)).astype(jnp.float32).astype(jnp.bfloat16)
    local = (sub16 // 2 % 2) * LANES + lane16
    inside = jnp.where(first_column + local + 2 * LANES < width - 1, 1.0, 0.0).astype(jnp.bfloat16)
    local8 = (sub8 // 2 % 2) * LANES + lane8
    limit = width - 1 - first_column
    sub_pair = sub8 // 2
    flat_tables = table_ref.reshape(3, quads, 2, 16, LANES)
    flat_even = even_ref.reshape(quads, 2, LANES, LANES)
    flat_plain = plain_ref.reshape(half, 2, LANES, LANES)

    def lower_masks(quad):
        bounds = [limit - orders_ref[my_owner * slots + g * quads + quad] for g in range(4)]
        pairs = [jnp.where(sub8 < 4, bounds[2 * p], bounds[2 * p + 1]) for p in range(2)]
        return [
            jnp.concatenate(
                [jnp.where(local8 + 2 * LANES * k < pair, 1.0, 0.0) for pair in pairs], axis=0
            ).astype(jnp.bfloat16)
            for k in range(2)
        ]

    def weighted(table, quad, masks):
        full = [flat_tables[table, quad, 0], flat_tables[table, quad, 1] * inside]
        low = [full[k] * masks[k] for k in range(2)]
        return [
            jnp.concatenate(pair, axis=1)
            for pair in (full, [v * alternate for v in full], low, [v * alternate for v in low])
        ]

    spin_pair = (lane8 // 32 % 2) * 2 + lane8 // 4 % 2
    plain_pair = (lane8 // 16 % 2) * 2 + lane8 // 4 % 2

    def spin_quad(quad, carry):
        masks = lower_masks(quad)
        left = jnp.concatenate(weighted(1, quad, masks) + weighted(2, quad, masks), axis=0)
        right = jnp.concatenate([flat_even[quad, 0], flat_even[quad, 1]], axis=1)
        product = lax.dot_general(left, right, NT, preferred_element_type=jnp.float32)
        for t in range(2):
            group = []
            for q in range(4):
                at = (t * 4 + q) * 16
                group.append(jnp.where(lane8 < 64, product[at : at + 8], product[at + 8 : at + 16]))
            spin_part[t, pl.ds(pl.multiple_of(quad * 8, 8), 8), :] = rotate_sums(
                group, spin_pair, sub_pair
            )
        return carry

    def plain_octet(octet, carry):
        parts = []
        for ab in range(2):
            quad = octet + ab * half
            parts.append(weighted(0, quad, lower_masks(quad)))
        left = jnp.concatenate([parts[ab][q] for q in range(4) for ab in range(2)], axis=0)
        right = jnp.concatenate([flat_plain[octet, 0], flat_plain[octet, 1]], axis=1)
        product = lax.dot_general(left, right, NT, preferred_element_type=jnp.float32)
        group = []
        for q in range(4):
            chosen = product[q * 32 : q * 32 + 8]
            for g in range(1, 4):
                at = q * 32 + g * 8
                chosen = jnp.where(lane8 // 32 == g, product[at : at + 8], chosen)
            group.append(chosen)
        plain_part[pl.ds(pl.multiple_of(octet * 8, 8), 8), :] = rotate_sums(
            group, plain_pair, sub_pair
        )
        return carry

    def exchange(piece, step):
        owner, source = shifted_device(step)
        return pltpu.make_async_remote_copy(
            src_ref=send_ref.at[piece, owner * sources + source],
            dst_ref=held_ref.at[piece, me],
            send_sem=send_sem.at[piece, step],
            recv_sem=recv_sem.at[piece, step],
            device_id=(owner, source),
            device_id_type=mesh_ids,
        )

    def send_piece(piece):
        def send(step, carry):
            exchange(piece, step).start()
            return carry

        lax.fori_loop(1, count, send, 0)
        held_ref[piece, me] = send_ref[piece, me]

    ordered = ordered_rows(my_owner)
    upper_sign = jnp.where(lane8 < 64, 1.0, (1 - 2 * (ordered % 2)).astype(jnp.float32))
    flat_send = send_ref.reshape(3, count * 8, LANES)

    def by_order(load, south):
        low = load(2 + south)
        return jnp.concatenate([low, load(south) - low], axis=0).T

    def spin_piece(piece, carry):
        def sub_block(sub, inner):
            for copy in spin_copies(sub):
                copy.wait()
            return lax.fori_loop(
                0, SUB, lambda i, c: spin_quad(sub * SUB + i, c), inner, unroll=SUB
            )

        for sub in range(half // SUB):
            sub_block(piece * (half // SUB) + sub, 0)
        first = piece * half * 8
        sign = jnp.where(piece == 0, upper_sign[0:4], upper_sign[4:8])
        for south in range(2):
            for r in range(2):
                plus, minus = (
                    by_order(lambda q: spin_part[t, pl.ds(first + q * 2 + r, half, stride=8), :], south)
                    for t in range(2)
                )
                if south:
                    minus = -minus
                for g in range(4):
                    at = g * 32
                    ep_re, ep_im, bp_re, bp_im = (plus[at + 8 * i : at + 8 * i + 8] for i in range(4))
                    em_re, em_im, bm_re, bm_im = (minus[at + 8 * i : at + 8 * i + 8] for i in range(4))
                    values = (bm_im - ep_re, -(ep_im + bm_re), -(bp_re + em_im), em_re - bp_im)
                    for i, value in enumerate(values):
                        value = value + pltpu.roll(value, 4, 0)
                        if south:
                            value = value * sign[g : g + 1, :]
                        row = ((south * 2 + r) * sources + (i // 2) * 4) * 8 + (i % 2) * 4 + g
                        flat_send[piece, pl.ds(row, 4, stride=8), :] = value[0:4]

        @pl.when(piece == 0)
        def _():
            pl.semaphore_wait(barrier, count - 1)

        send_piece(piece)
        return carry

    lax.fori_loop(0, 2, spin_piece, 0)

    def plain_block(sub, carry):
        for copy in plain_copies(sub):
            copy.wait()
        return lax.fori_loop(
            0, SUB, lambda i, c: plain_octet(sub * SUB + i, c), carry, unroll=SUB
        )

    lax.fori_loop(0, plain_subs, plain_block, 0)
    for south in range(2):
        for r in range(2):
            turned = by_order(lambda q: plain_part[pl.ds(q * 2 + r, half, stride=8), :], south)
            for k in range(8):
                real, imag = turned[k * 16 : k * 16 + 8], turned[k * 16 + 8 : k * 16 + 16]
                value = jnp.where(
                    sub8 < 4, real + pltpu.roll(real, 4, 0), imag + pltpu.roll(imag, 4, 0)
                )
                if south:
                    value = value * upper_sign[k : k + 1, :]
                row = (south * 2 + r) * sources * 8 + k
                flat_send[2, pl.ds(row, 8, stride=8), :] = value
    send_piece(2)
    for copy in small[2:]:
        copy.wait()

    tall = width // LANES
    tall_ids = lax.broadcasted_iota(jnp.int32, (tall, LANES), 0)

    def received(piece, near):
        def await_step(step, carry):
            exchange(piece, step).wait()
            return carry

        lax.fori_loop(max(1, near * sources), (near + 1) * sources, await_step, 0)
        owner = lax.rem(my_owner + owners - near, owners)
        total = held_ref[piece, owner * sources]
        for source in range(1, sources):
            total = total + held_ref[piece, owner * sources + source]
        high = total.astype(jnp.bfloat16).astype(jnp.float32)
        rest = total - high
        middle = rest.astype(jnp.bfloat16).astype(jnp.float32)
        return ordered_rows(owner), (high, middle, rest - middle)

    def place(ordered_row, pieces, row, left_row, at):
        here = tall_ids == ordered_row // LANES
        for i in range(3):
            to = left_row + i * tall
            left_ref[to : to + tall, at * LANES : (at + 1) * LANES] = jnp.where(
                here, pieces[i][row : row + 1, :], 0.0
            ).astype(jnp.bfloat16)

    def place_spin(piece):
        for near in range(owners):
            ordered, pieces = received(piece, near)
            for g in range(4):
                at = (piece * owners + near) * 4 + g
                for part in range(2):
                    place(
                        ordered[piece * 4 + g : piece * 4 + g + 1, :],
                        pieces, part * 4 + g, part * 3 * tall, at,
                    )
        span = pl.ds(piece * owners * 4 * LANES, owners * 4 * LANES)
        return lax.dot_general(
            left_ref[0 : 6 * tall, span], right_ref[:, span], NT, preferred_element_type=jnp.float32
        )

    def joined(placed, at):
        return placed[at : at + tall] + placed[at + tall : at + 2 * tall] + placed[at + 2 * tall : at + 3 * tall]

    wide = 2 * tall

    def pixel_copy(which, step):
        source = lax.rem(my_source + step, sources)
        return pltpu.make_async_remote_copy(
            src_ref=pixel_ref.at[which, source],
            dst_ref=landed_ref.at[which, my_source],
            send_sem=pixel_send.at[which, step],
            recv_sem=pixel_recv.at[which, step],
            device_id=(my_owner, source),
            device_id_type=mesh_ids,
        )

    def transform(which, real_part, imag_part):
        spectrum = jnp.concatenate([real_part, imag_part], axis=0)
        first = jnp.dot(
            first_ref[...], spectrum, precision=highest, preferred_element_type=jnp.float32
        )
        real, imag = first[:wide], first[wide:]
        twisted = jnp.concatenate(
            [
                real * twist_ref[0] - imag * twist_ref[1],
                real * twist_ref[1] + imag * twist_ref[0],
            ],
            axis=1,
        )
        both = lax.dot_general(
            last_ref[...], twisted, NT, precision=highest, preferred_element_type=jnp.float32
        )
        pixels = jnp.concatenate([both[:wide], both[wide:]], axis=1)
        for e in range(sources):
            pixel_ref[which, e] = pixels[e * 8 : e * 8 + 8]
        for step in range(1, sources):
            pixel_copy(which, step).start()
        landed_ref[which, my_source] = pixel_ref[which, my_source]

    shifted = cycle_ref[lax.rem(my_owner, cycle_ref.shape[0])] % 2 == 1
    factor = phase_ref[2]
    cosine = jnp.where(shifted, phase_ref[0], factor)
    sine = jnp.where(shifted, phase_ref[1], 0.0)

    placed = place_spin(0)
    placed = placed + place_spin(1)
    real, imag = joined(placed, 0), joined(placed, 3 * tall)
    transform(0, real * cosine - imag * sine, real * sine + imag * cosine)

    for near in range(owners):
        ordered, pieces = received(2, near)
        for k in range(8):
            at = ((k // 4) * owners + near) * 4 + k % 4
            place(ordered[k : k + 1, :], pieces, k, 0, at)
    placed = lax.dot_general(
        left_ref[0 : 3 * tall, :], right_ref[...], NT, preferred_element_type=jnp.float32
    )
    value = joined(placed, 0)
    is_real = my_source < sources // 2
    transform(1, value * jnp.where(is_real, cosine, -sine), value * jnp.where(is_real, sine, cosine))
    for which in range(2):
        for step in range(1, sources):
            pixel_copy(which, step).wait()
    for c in range(4):
        out_ref[c] = landed_ref[1, c] + landed_ref[1, 4 + c]
        out_ref[4 + c] = landed_ref[0, c]
        out_ref[8 + c] = landed_ref[0, 4 + c]


def synthesis_tables(orders_count):
    pixels = 2 * orders_count
    tall = orders_count // LANES
    half = 2 * tall
    orders = np.arange(orders_count).reshape(tall, LANES)
    factor = np.where(orders == 0, 1.0, 2.0)
    angle = orders * (np.pi / pixels)
    phase = np.stack([np.cos(angle) * factor, np.sin(angle) * factor, factor])
    angle = (np.arange(half)[:, None] * np.arange(tall)[None, :] % half) * (2 * np.pi / half)
    first = np.block([[np.cos(angle), -np.sin(angle)], [np.sin(angle), np.cos(angle)]])
    angle = np.arange(half)[:, None] * np.arange(LANES)[None, :] * (2 * np.pi / pixels)
    twist = np.stack([np.cos(angle), np.sin(angle)])
    ids = np.concatenate([np.arange(0, LANES, 2), np.arange(1, LANES, 2)])
    angle = (ids[:, None] * np.arange(LANES)[None, :] % LANES) * (2 * np.pi / LANES)
    last = np.concatenate([np.cos(angle), -np.sin(angle)], axis=1)
    return [jnp.asarray(t, jnp.float32) for t in (phase, first, twist, last)]


def packed_body(legendre, harmonics, slot_orders, cycle_index):
    owners, sources = lax.axis_size("ma"), lax.axis_size("ell")
    slots, columns = harmonics.shape[0], harmonics.shape[-1]
    width = 2 * slot_orders.shape[0]
    quads, tall, count = slots // 4, width // LANES, owners * sources
    tables = (
        legendre.reshape(3, slots, 2, 4, LANES)
        .transpose(0, 1, 3, 2, 4)
        .reshape(3, 4, quads, 2, 4, LANES)
    )
    packed = (
        harmonics.reshape(slots, 3, 2, 4, 4, LANES)
        .transpose(0, 1, 2, 4, 3, 5)
        .reshape(4, quads, 6, 2, 8, LANES)
    )
    constants = synthesis_tables(width)
    anywhere = pl.BlockSpec(memory_space=pl.ANY)
    dma = pltpu.SemaphoreType.DMA
    maps = pl.pallas_call(
        functools.partial(fused_kernel, width, slots, columns),
        in_specs=[anywhere] * 9,
        out_specs=pl.BlockSpec(memory_space=pltpu.VMEM),
        out_shape=jax.ShapeDtypeStruct((12, 8, LANES), jnp.float32),
        scratch_shapes=[
            pltpu.SMEM(cycle_index.shape, jnp.int32),
            pltpu.SMEM(slot_orders.shape, jnp.int32),
            pltpu.VMEM((owners, 4, LANES), jnp.int32),
            pltpu.VMEM((3, quads, 2, 4, 4, LANES), jnp.bfloat16),
            pltpu.VMEM((quads, 2, 4, 4, 8, LANES), jnp.bfloat16),
            pltpu.VMEM((quads // 2, 2, 2, 4, 2, 8, LANES), jnp.bfloat16),
            *(pltpu.VMEM(c.shape, c.dtype) for c in constants),
            pltpu.VMEM((2, quads * 8, LANES), jnp.float32),
            pltpu.VMEM((quads * 4, LANES), jnp.float32),
            pltpu.VMEM((3, count, 8, LANES), jnp.float32),
            pltpu.VMEM((3, count, 8, LANES), jnp.float32),
            pltpu.VMEM((6 * tall, width), jnp.bfloat16),
            pltpu.VMEM((LANES, width), jnp.bfloat16),
            pltpu.VMEM((2, sources, 8, LANES), jnp.float32),
            pltpu.VMEM((2, sources, 8, LANES), jnp.float32),
            dma((7,)),
            dma((quads // SUB, 12)),
            dma((quads // 2 // SUB, 24)),
            dma((3, count)),
            dma((3, count)),
            dma((2, sources)),
            dma((2, sources)),
        ],
        compiler_params=pltpu.CompilerParams(
            vmem_limit_bytes=60 * 1024 * 1024, collective_id=0, has_side_effects=True
        ),
    )(cycle_index, slot_orders, slot_orders.reshape(owners, 4, LANES), tables, packed, *constants)
    return maps.reshape(1, 3, 4, 8 * LANES)


def body(legendre, harmonics, slot_orders, cycle_index):
    owners, sources = lax.axis_size("ma"), lax.axis_size("ell")
    slots, kinds, parts, components, columns = harmonics.shape
    pairs = cycle_index.shape[0]
    fits = (
        (pairs, components, columns, slots) == (2, 4, 4 * LANES, 4 * LANES)
        and owners == 2 * pairs
        and kinds * parts * components == 3 * sources
        and slot_orders.shape[0] * 4 == sources * 8 * LANES
    )
    chosen = packed_body if fits else general_body
    return chosen(legendre, harmonics, slot_orders, cycle_index)


def solution(mesh):
    return jax.shard_map(
        body,
        mesh=mesh,
        in_specs=(P(None, "ma", None, "ell"), P("ma", None, None, None, "ell"), P(), P()),
        out_specs=P("ma", None, None, "ell"),
        check_vma=False,
    )
```

profile of v0, /device:TPU:0, one launch (start us, length us, event | category | flops | bytes accessed | tf_op | source)
XLA Modules:
  0.0 29.9 jit_solution(11457681708960468948)
XLA Ops:
  0.0 28.4 %shard_map.82 = f32[12,8,128]{2,1,0:T(8,128)} custom-call(s32[2]{0:T(128)} %cycle_hbm.1, s32[2048]{0:T(1024)} %orders_hbm.1, s32[4,4,128]{2,1,0:T(4,128)} %bitcast.13, bf16[3,4,128,2,4,128]{5,4,3,2,1,0:T(4,128)(2,1)} %bitcast.12, bf16[4,128,6,2,8,128]{5,4,3,2,1,0:T(8,128)(2,1)} %bitcast.11, f32[3,32,128]{2,1,0:T(8,128)} %constant.8.clone.phase_hbm, ...), custom_call_target="tpu_custom_call" | custom-call | tf_op jit(solution)/shard_map/pallas_call | solution.py:608
  28.5 1.4 %reshape.23 = f32[1,3,4,1024]{3,2,1,0:T(4,128)} reshape(f32[12,8,128]{2,1,0:T(8,128)} %shard_map.82) | data formatting | bytes 98304 | tf_op jit(solution)/shard_map/reshape | solution.py:641
where the time goes:
time: 30.1 us; the launch traced here: 29.9 us
  Pallas kernels  28.4 us (94%)
  local copies, waits for them, and re-layouts  1.44 us (5%)
    pallas_call x1, Pallas kernels, packed_body(): pl.pallas_call(functools.partial(fused_kernel, width, slots, columns), in...  28.4 us
    reshape x1, local copies, waits for them, and re-layouts, packed_body(): return maps.reshape(1, 3, 4, 8 * LANES)  1.44 us

commit v1 on v0

--- a/solution.py
+++ b/solution.py
@@ -186,15 +186,13 @@
     phase_hbm, first_hbm, twist_hbm, last_hbm, out_ref,
     cycle_ref, orders_ref, rows_ref, table_ref, even_ref, plain_ref,
     phase_ref, first_ref, twist_ref, last_ref,
-    spin_part, plain_part, send_ref, held_ref, left_ref, right_ref, pixel_ref, landed_ref,
-    small_sem, spin_sem, plain_sem, send_sem, recv_sem, pixel_send, pixel_recv,
+    spin_part, plain_part, send_ref, fold_ref, half_ref, held_ref, left_ref, right_ref, pixel_ref, landed_ref,
+    small_sem, spin_sem, plain_sem, fold_send, fold_recv, send_sem, recv_sem, pixel_send, pixel_recv,
 ):
     highest = lax.Precision.HIGHEST
     owners, sources = lax.axis_size("ma"), lax.axis_size("ell")
     my_owner, my_source = lax.axis_index("ma"), lax.axis_index("ell")
-    me = my_owner * sources + my_source
     mesh_ids = pl.DeviceIdType.MESH
-    count = owners * sources
     quads = slots // 4
     half = quads // 2
     subs = quads // SUB
@@ -257,20 +255,25 @@
     for copy in small[2:]:
         copy.start()
 
+    def wrapped(place, step, size):
+        place = place + step
+        return jnp.where(place >= size, place - size, place)
+
+    lines = sources // 2
+    my_line, my_side = my_source // 2, my_source % 2
+    near_owner = [wrapped(my_owner, i, owners) for i in range(owners)]
+    near_line = [wrapped(my_line, i, lines) for i in range(lines)]
+    spread = owners * lines
+
     def shifted_device(step):
-        owner = lax.rem(my_owner + step // sources, owners)
-        source = lax.rem(my_source + step % sources, sources)
-        return owner, source
+        return near_owner[step // lines], near_line[step % lines] * 2 + my_side
 
     barrier = pltpu.get_barrier_semaphore()
 
-    def greet(step, carry):
-        pl.semaphore_signal(
-            barrier, inc=1, device_id=shifted_device(step), device_id_type=mesh_ids
-        )
-        return carry
-
-    lax.fori_loop(1, count, greet, 0)
+    met = [shifted_device(step) for step in range(1, spread)]
+    met += [(my_owner, near_line[i] * 2 + 1 - my_side) for i in range(lines)]
+    for device in reversed(met):
+        pl.semaphore_signal(barrier, inc=1, device_id=device, device_id_type=mesh_ids)
 
     lane8 = lax.broadcasted_iota(jnp.int32, (8, LANES), 1)
     sub8 = lax.broadcasted_iota(jnp.int32, (8, LANES), 0)
@@ -289,15 +292,6 @@
             axis=0,
         )
 
-    lane_rows = lax.broadcasted_iota(jnp.int32, (LANES, LANES), 0)
-    for near in range(owners):
-        ordered = ordered_rows(lax.rem(my_owner + owners - near, owners))
-        for k in range(8):
-            at = ((k // 4) * owners + near) * 4 + k % 4
-            right_ref[:, at * LANES : (at + 1) * LANES] = jnp.where(
-                lane_rows == ordered[k : k + 1, :] % LANES, 1.0, 0.0
-            ).astype(jnp.bfloat16)
-
     first_column = my_source * columns
     lane16 = lax.broadcasted_iota(jnp.int32, (16, LANES), 1)
     sub16 = lax.broadcasted_iota(jnp.int32, (16, LANES), 0)
@@ -307,7 +301,6 @@
     local8 = (sub8 // 2 % 2) * LANES + lane8
     limit = width - 1 - first_column
     sub_pair = sub8 // 2
-    flat_tables = table_ref.reshape(3, quads, 2, 16, LANES)
     flat_even = even_ref.reshape(quads, 2, LANES, LANES)
     flat_plain = plain_ref.reshape(half, 2, LANES, LANES)
 
@@ -322,7 +315,11 @@
         ]
 
     def weighted(table, quad, masks):
-        full = [flat_tables[table, quad, 0], flat_tables[table, quad, 1] * inside]
+        full = [
+            jnp.concatenate([table_ref[table, quad, k, g] for g in range(4)], axis=0)
+            for k in range(2)
+        ]
+        full[1] = full[1] * inside
         low = [full[k] * masks[k] for k in range(2)]
         return [
             jnp.concatenate(pair, axis=1)
@@ -367,43 +364,47 @@
         )
         return carry
 
+    def fold(piece):
+        return pltpu.make_async_remote_copy(
+            src_ref=send_ref.at[piece, :, 1 - my_side],
+            dst_ref=fold_ref.at[piece],
+            send_sem=fold_send.at[piece],
+            recv_sem=fold_recv.at[piece],
+            device_id=(my_owner, my_line * 2 + 1 - my_side),
+            device_id_type=mesh_ids,
+        )
+
     def exchange(piece, step):
-        owner, source = shifted_device(step)
+        owner, line = near_owner[step // lines], near_line[step % lines]
         return pltpu.make_async_remote_copy(
-            src_ref=send_ref.at[piece, owner * sources + source],
-            dst_ref=held_ref.at[piece, me],
+            src_ref=half_ref.at[piece, owner, line],
+            dst_ref=held_ref.at[piece, my_owner, my_line],
             send_sem=send_sem.at[piece, step],
             recv_sem=recv_sem.at[piece, step],
-            device_id=(owner, source),
+            device_id=(owner, line * 2 + my_side),
             device_id_type=mesh_ids,
         )
 
-    def send_piece(piece):
-        def send(step, carry):
+    def forward_piece(piece):
+        fold(piece).wait_recv()
+        for owner in range(owners):
+            for line in range(lines):
+                half_ref[piece, owner, line] = (
+                    send_ref[piece, owner, my_side, line] + fold_ref[piece, owner, line]
+                )
+        for step in range(1, spread):
             exchange(piece, step).start()
-            return carry
-
-        lax.fori_loop(1, count, send, 0)
-        held_ref[piece, me] = send_ref[piece, me]
+        held_ref[piece, my_owner, my_line] = half_ref[piece, my_owner, my_line]
 
     ordered = ordered_rows(my_owner)
     upper_sign = jnp.where(lane8 < 64, 1.0, (1 - 2 * (ordered % 2)).astype(jnp.float32))
-    flat_send = send_ref.reshape(3, count * 8, LANES)
+    flat_send = send_ref.reshape(3, owners * sources * 8, LANES)
 
     def by_order(load, south):
         low = load(2 + south)
         return jnp.concatenate([low, load(south) - low], axis=0).T
 
-    def spin_piece(piece, carry):
-        def sub_block(sub, inner):
-            for copy in spin_copies(sub):
-                copy.wait()
-            return lax.fori_loop(
-                0, SUB, lambda i, c: spin_quad(sub * SUB + i, c), inner, unroll=SUB
-            )
-
-        for sub in range(half // SUB):
-            sub_block(piece * (half // SUB) + sub, 0)
+    def finish_spin(piece):
         first = piece * half * 8
         sign = jnp.where(piece == 0, upper_sign[0:4], upper_sign[4:8])
         for south in range(2):
@@ -426,16 +427,32 @@
                         row = ((south * 2 + r) * sources + (i // 2) * 4) * 8 + (i % 2) * 4 + g
                         flat_send[piece, pl.ds(row, 4, stride=8), :] = value[0:4]
 
-        @pl.when(piece == 0)
+    per_piece = half // SUB
+
+    def spin_block(sub, carry):
+        for copy in spin_copies(sub):
+            copy.wait()
+        lax.fori_loop(0, SUB, lambda i, c: spin_quad(sub * SUB + i, c), 0, unroll=SUB)
+
+        @pl.when(lax.rem(sub, per_piece) == per_piece - 1)
         def _():
-            pl.semaphore_wait(barrier, count - 1)
-
-        send_piece(piece)
+            finish_spin(lax.div(sub, per_piece))
+
+        @pl.when(sub == per_piece)
+        def _():
+            pl.semaphore_wait(barrier, len(met))
+            fold(0).start()
+
         return carry
 
-    lax.fori_loop(0, 2, spin_piece, 0)
+    lax.fori_loop(0, subs, spin_block, 0)
+    fold(1).start()
 
     def plain_block(sub, carry):
+        @pl.when(sub == plain_subs - 1)
+        def _():
+            forward_piece(0)
+
         for copy in plain_copies(sub):
             copy.wait()
         return lax.fori_loop(
@@ -455,23 +472,30 @@
                     value = value * upper_sign[k : k + 1, :]
                 row = (south * 2 + r) * sources * 8 + k
                 flat_send[2, pl.ds(row, 8, stride=8), :] = value
-    send_piece(2)
+    fold(2).start()
+    forward_piece(1)
+    lane_rows = lax.broadcasted_iota(jnp.int32, (LANES, LANES), 0)
+    for near in range(owners):
+        ordered = ordered_rows(lax.rem(my_owner + owners - near, owners))
+        for k in range(8):
+            at = ((k // 4) * owners + near) * 4 + k % 4
+            right_ref[:, at * LANES : (at + 1) * LANES] = jnp.where(
+                lane_rows == ordered[k : k + 1, :] % LANES, 1.0, 0.0
+            ).astype(jnp.bfloat16)
     for copy in small[2:]:
         copy.wait()
+    forward_piece(2)
 
     tall = width // LANES
     tall_ids = lax.broadcasted_iota(jnp.int32, (tall, LANES), 0)
 
     def received(piece, near):
-        def await_step(step, carry):
+        for step in range(max(1, near * lines), (near + 1) * lines):
             exchange(piece, step).wait()
-            return carry
-
-        lax.fori_loop(max(1, near * sources), (near + 1) * sources, await_step, 0)
         owner = lax.rem(my_owner + owners - near, owners)
-        total = held_ref[piece, owner * sources]
-        for source in range(1, sources):
-            total = total + held_ref[piece, owner * sources + source]
+        total = held_ref[piece, owner, 0]
+        for line in range(1, lines):
+            total = total + held_ref[piece, owner, line]
         high = total.astype(jnp.bfloat16).astype(jnp.float32)
         rest = total - high
         middle = rest.astype(jnp.bfloat16).astype(jnp.float32)
@@ -558,15 +582,17 @@
         left_ref[0 : 3 * tall, :], right_ref[...], NT, preferred_element_type=jnp.float32
     )
     value = joined(placed, 0)
-    is_real = my_source < sources // 2
+    is_real = my_side == 0
     transform(1, value * jnp.where(is_real, cosine, -sine), value * jnp.where(is_real, sine, cosine))
+    for piece in range(3):
+        fold(piece).wait_send()
     for which in range(2):
         for step in range(1, sources):
             pixel_copy(which, step).wait()
     for c in range(4):
-        out_ref[c] = landed_ref[1, c] + landed_ref[1, 4 + c]
-        out_ref[4 + c] = landed_ref[0, c]
-        out_ref[8 + c] = landed_ref[0, 4 + c]
+        out_ref[c] = landed_ref[1, 2 * c] + landed_ref[1, 2 * c + 1]
+        out_ref[4 + c] = landed_ref[0, 2 * c]
+        out_ref[8 + c] = landed_ref[0, 2 * c + 1]
 
 
 def synthesis_tables(orders_count):
@@ -591,7 +617,7 @@
     owners, sources = lax.axis_size("ma"), lax.axis_size("ell")
     slots, columns = harmonics.shape[0], harmonics.shape[-1]
     width = 2 * slot_orders.shape[0]
-    quads, tall, count = slots // 4, width // LANES, owners * sources
+    quads, tall, lines = slots // 4, width // LANES, sources // 2
     tables = (
         legendre.reshape(3, slots, 2, 4, LANES)
         .transpose(0, 1, 3, 2, 4)
@@ -603,6 +629,12 @@
         .reshape(4, quads, 6, 2, 8, LANES)
     )
     constants = synthesis_tables(width)
+    operands = [
+        pltpu.with_memory_space_constraint(x, pltpu.HBM)
+        for x in (
+            cycle_index, slot_orders, slot_orders.reshape(owners, 4, LANES), tables, packed, *constants
+        )
+    ]
     anywhere = pl.BlockSpec(memory_space=pl.ANY)
     dma = pltpu.SemaphoreType.DMA
     maps = pl.pallas_call(
@@ -620,8 +652,10 @@
             *(pltpu.VMEM(c.shape, c.dtype) for c in constants),
             pltpu.VMEM((2, quads * 8, LANES), jnp.float32),
             pltpu.VMEM((quads * 4, LANES), jnp.float32),
-            pltpu.VMEM((3, count, 8, LANES), jnp.float32),
-            pltpu.VMEM((3, count, 8, LANES), jnp.float32),
+            pltpu.VMEM((3, owners, 2, lines, 8, LANES), jnp.float32),
+            pltpu.VMEM((3, owners, lines, 8, LANES), jnp.float32),
+            pltpu.VMEM((3, owners, lines, 8, LANES), jnp.float32),
+            pltpu.VMEM((3, owners, lines, 8, LANES), jnp.float32),
             pltpu.VMEM((6 * tall, width), jnp.bfloat16),
             pltpu.VMEM((LANES, width), jnp.bfloat16),
             pltpu.VMEM((2, sources, 8, LANES), jnp.float32),
@@ -629,15 +663,17 @@
             dma((7,)),
             dma((quads // SUB, 12)),
             dma((quads // 2 // SUB, 24)),
-            dma((3, count)),
-            dma((3, count)),
+            dma((3,)),
+            dma((3,)),
+            dma((3, owners * lines)),
+            dma((3, owners * lines)),
             dma((2, sources)),
             dma((2, sources)),
         ],
         compiler_params=pltpu.CompilerParams(
-            vmem_limit_bytes=60 * 1024 * 1024, collective_id=0, has_side_effects=True
+            vmem_limit_bytes=40 * 1024 * 1024, collective_id=0, has_side_effects=True
         ),
-    )(cycle_index, slot_orders, slot_orders.reshape(owners, 4, LANES), tables, packed, *constants)
+    )(*operands)
     return maps.reshape(1, 3, 4, 8 * LANES)
 
 

time: 30.1 us -> 27.9 us (0.927)
  Pallas kernels: 28.4 us -> 27.1 us
  local copies, waits for them, and re-layouts: 1.44 us -> 0.64 us
    pallas_call x1, Pallas kernels: 28.4 us -> 27.1 us  [packed_body(): pl.pallas_call(functools.partial(fused_kernel, width, slots, columns), in...]
    reshape x1, local copies, waits for them, and re-layouts: 1.44 us -> 0.64 us  [packed_body(): return maps.reshape(1, 3, 4, 8 * LANES)]
where the time goes in v1:
time: 27.9 us; the launch traced here: 27.7 us
  Pallas kernels  27.1 us (97%)
  local copies, waits for them, and re-layouts  0.64 us (2%)
    pallas_call x1, Pallas kernels, packed_body(): pl.pallas_call(functools.partial(fused_kernel, width, slots, columns), in...  27.1 us
    reshape x1, local copies, waits for them, and re-layouts, packed_body(): return maps.reshape(1, 3, 4, 8 * LANES)  0.64 us

profile of v1, /device:TPU:0, one launch (start us, length us, event | category | flops | bytes accessed | tf_op | source)
XLA Modules:
  0.0 27.7 jit_solution(12667732724823626537)
XLA Ops:
  0.0 27.1 %shard_map.82 = f32[12,8,128]{2,1,0:T(8,128)S(1)} custom-call(s32[2]{0:T(128)} %cycle_hbm.1, s32[2048]{0:T(1024)} %orders_hbm.1, s32[4,4,128]{2,1,0:T(4,128)} %bitcast.13, bf16[3,4,128,2,4,128]{5,4,3,2,1,0:T(4,128)(2,1)} %bitcast.12, bf16[4,128,6,2,8,128]{5,4,3,2,1,0:T(8,128)(2,1)} %bitcast.11, f32[3,32,128]{2,1,0:T(8,128)} %constant.8.clone.phase_hbm, ...), custom_call_target="tpu_custom_call" | custom-call | tf_op jit(solution)/shard_map/pallas_call | solution.py:640
  27.1 0.6 %reshape.23 = f32[1,3,4,1024]{3,2,1,0:T(4,128)} reshape(f32[12,8,128]{2,1,0:T(8,128)S(1)} %shard_map.82) | data formatting | bytes 98304 | tf_op jit(solution)/shard_map/reshape | solution.py:677

commit v2 on v1

--- a/solution.py
+++ b/solution.py
@@ -186,10 +186,9 @@
     phase_hbm, first_hbm, twist_hbm, last_hbm, out_ref,
     cycle_ref, orders_ref, rows_ref, table_ref, even_ref, plain_ref,
     phase_ref, first_ref, twist_ref, last_ref,
-    spin_part, plain_part, send_ref, fold_ref, half_ref, held_ref, left_ref, right_ref, pixel_ref, landed_ref,
-    small_sem, spin_sem, plain_sem, fold_send, fold_recv, send_sem, recv_sem, pixel_send, pixel_recv,
+    spin_part, plain_part, send_ref, held_ref, left_ref, right_ref, pixel_ref, landed_ref,
+    small_sem, spin_sem, plain_sem, send_sem, recv_sem, pixel_send, pixel_recv,
 ):
-    highest = lax.Precision.HIGHEST
     owners, sources = lax.axis_size("ma"), lax.axis_size("ell")
     my_owner, my_source = lax.axis_index("ma"), lax.axis_index("ell")
     mesh_ids = pl.DeviceIdType.MESH
@@ -237,6 +236,36 @@
             pltpu.make_async_copy(a, b, plain_sem.at[sub, i]) for i, (a, b) in enumerate(copies)
         ]
 
+    def wrapped(place, step, size):
+        place = place + step
+        return jnp.where(place >= size, place - size, place)
+
+    lines = sources // 2
+    my_line, my_side = my_source // 2, my_source % 2
+    near_owner = [wrapped(my_owner, i, owners) for i in range(owners)]
+    near_line = [wrapped(my_line, i, lines) for i in range(lines)]
+    rising = my_line * 2 >= lines
+    far_line = [
+        wrapped(my_line, jnp.where(rising, i, lines - i), lines) for i in range(1, lines)
+    ]
+    far_line.append(my_line)
+    far_owner = [near_owner[i] for i in (*range(1, owners), 0)]
+    others = [
+        (owner, line, side)
+        for i, line in enumerate(far_line)
+        for side in (1 - my_side, my_side)
+        for j, owner in enumerate(far_owner)
+        if (i, side is my_side, j) != (lines - 1, True, owners - 1)
+    ]
+    same_owner = [d for d in others if d[0] is near_owner[0]]
+
+    barrier = pltpu.get_barrier_semaphore()
+
+    for owner, line, side in others:
+        pl.semaphore_signal(
+            barrier, inc=1, device_id=(owner, line * 2 + side), device_id_type=mesh_ids
+        )
+
     small[0].start()
     small[1].start()
 
@@ -254,26 +283,6 @@
     lax.fori_loop(0, plain_subs, start_plain, 0)
     for copy in small[2:]:
         copy.start()
-
-    def wrapped(place, step, size):
-        place = place + step
-        return jnp.where(place >= size, place - size, place)
-
-    lines = sources // 2
-    my_line, my_side = my_source // 2, my_source % 2
-    near_owner = [wrapped(my_owner, i, owners) for i in range(owners)]
-    near_line = [wrapped(my_line, i, lines) for i in range(lines)]
-    spread = owners * lines
-
-    def shifted_device(step):
-        return near_owner[step // lines], near_line[step % lines] * 2 + my_side
-
-    barrier = pltpu.get_barrier_semaphore()
-
-    met = [shifted_device(step) for step in range(1, spread)]
-    met += [(my_owner, near_line[i] * 2 + 1 - my_side) for i in range(lines)]
-    for device in reversed(met):
-        pl.semaphore_signal(barrier, inc=1, device_id=device, device_id_type=mesh_ids)
 
     lane8 = lax.broadcasted_iota(jnp.int32, (8, LANES), 1)
     sub8 = lax.broadcasted_iota(jnp.int32, (8, LANES), 0)
@@ -364,37 +373,21 @@
         )
         return carry
 
-    def fold(piece):
+    def exchange(piece, to, origin):
+        owner, line, side = to
         return pltpu.make_async_remote_copy(
-            src_ref=send_ref.at[piece, :, 1 - my_side],
-            dst_ref=fold_ref.at[piece],
-            send_sem=fold_send.at[piece],
-            recv_sem=fold_recv.at[piece],
-            device_id=(my_owner, my_line * 2 + 1 - my_side),
+            src_ref=send_ref.at[piece, owner, side, line],
+            dst_ref=held_ref.at[piece, my_owner, my_side, my_line],
+            send_sem=send_sem.at[piece, owner, side, line],
+            recv_sem=recv_sem.at[(piece, *origin)],
+            device_id=(owner, line * 2 + side),
             device_id_type=mesh_ids,
         )
 
-    def exchange(piece, step):
-        owner, line = near_owner[step // lines], near_line[step % lines]
-        return pltpu.make_async_remote_copy(
-            src_ref=half_ref.at[piece, owner, line],
-            dst_ref=held_ref.at[piece, my_owner, my_line],
-            send_sem=send_sem.at[piece, step],
-            recv_sem=recv_sem.at[piece, step],
-            device_id=(owner, line * 2 + my_side),
-            device_id_type=mesh_ids,
-        )
-
-    def forward_piece(piece):
-        fold(piece).wait_recv()
-        for owner in range(owners):
-            for line in range(lines):
-                half_ref[piece, owner, line] = (
-                    send_ref[piece, owner, my_side, line] + fold_ref[piece, owner, line]
-                )
-        for step in range(1, spread):
-            exchange(piece, step).start()
-        held_ref[piece, my_owner, my_line] = half_ref[piece, my_owner, my_line]
+    def send_piece(piece):
+        for device in others:
+            exchange(piece, device, (my_owner, my_side, my_line)).start()
+        held_ref[piece, my_owner, my_side, my_line] = send_ref[piece, my_owner, my_side, my_line]
 
     ordered = ordered_rows(my_owner)
     upper_sign = jnp.where(lane8 < 64, 1.0, (1 - 2 * (ordered % 2)).astype(jnp.float32))
@@ -438,21 +431,17 @@
         def _():
             finish_spin(lax.div(sub, per_piece))
 
-        @pl.when(sub == per_piece)
+        @pl.when(sub == per_piece - 1)
         def _():
-            pl.semaphore_wait(barrier, len(met))
-            fold(0).start()
+            pl.semaphore_wait(barrier, len(others))
+            send_piece(0)
 
         return carry
 
     lax.fori_loop(0, subs, spin_block, 0)
-    fold(1).start()
+    send_piece(1)
 
     def plain_block(sub, carry):
-        @pl.when(sub == plain_subs - 1)
-        def _():
-            forward_piece(0)
-
         for copy in plain_copies(sub):
             copy.wait()
         return lax.fori_loop(
@@ -472,8 +461,7 @@
                     value = value * upper_sign[k : k + 1, :]
                 row = (south * 2 + r) * sources * 8 + k
                 flat_send[2, pl.ds(row, 8, stride=8), :] = value
-    fold(2).start()
-    forward_piece(1)
+    send_piece(2)
     lane_rows = lax.broadcasted_iota(jnp.int32, (LANES, LANES), 0)
     for near in range(owners):
         ordered = ordered_rows(lax.rem(my_owner + owners - near, owners))
@@ -484,26 +472,29 @@
             ).astype(jnp.bfloat16)
     for copy in small[2:]:
         copy.wait()
-    forward_piece(2)
 
     tall = width // LANES
     tall_ids = lax.broadcasted_iota(jnp.int32, (tall, LANES), 0)
 
+    def split(total):
+        high = total.astype(jnp.bfloat16).astype(jnp.float32)
+        return high, total - high
+
     def received(piece, near):
-        for step in range(max(1, near * lines), (near + 1) * lines):
-            exchange(piece, step).wait()
-        owner = lax.rem(my_owner + owners - near, owners)
-        total = held_ref[piece, owner, 0]
+        owner = near_owner[-near % owners]
+        for i in range(lines):
+            for side in (my_side, 1 - my_side):
+                if near or i or side is not my_side:
+                    device = (owner, near_line[i], side)
+                    exchange(piece, device, (owner, side, near_line[i])).wait_recv()
+        total = held_ref[piece, owner, 0, 0] + held_ref[piece, owner, 1, 0]
         for line in range(1, lines):
-            total = total + held_ref[piece, owner, line]
-        high = total.astype(jnp.bfloat16).astype(jnp.float32)
-        rest = total - high
-        middle = rest.astype(jnp.bfloat16).astype(jnp.float32)
-        return ordered_rows(owner), (high, middle, rest - middle)
+            total = total + held_ref[piece, owner, 0, line] + held_ref[piece, owner, 1, line]
+        return ordered_rows(owner), split(total)
 
     def place(ordered_row, pieces, row, left_row, at):
         here = tall_ids == ordered_row // LANES
-        for i in range(3):
+        for i in range(2):
             to = left_row + i * tall
             left_ref[to : to + tall, at * LANES : (at + 1) * LANES] = jnp.where(
                 here, pieces[i][row : row + 1, :], 0.0
@@ -517,34 +508,37 @@
                 for part in range(2):
                     place(
                         ordered[piece * 4 + g : piece * 4 + g + 1, :],
-                        pieces, part * 4 + g, part * 3 * tall, at,
+                        pieces, part * 4 + g, part * 2 * tall, at,
                     )
         span = pl.ds(piece * owners * 4 * LANES, owners * 4 * LANES)
         return lax.dot_general(
-            left_ref[0 : 6 * tall, span], right_ref[:, span], NT, preferred_element_type=jnp.float32
+            left_ref[0 : 4 * tall, span], right_ref[:, span], NT, preferred_element_type=jnp.float32
         )
 
     def joined(placed, at):
-        return placed[at : at + tall] + placed[at + tall : at + 2 * tall] + placed[at + 2 * tall : at + 3 * tall]
+        return placed[at : at + tall] + placed[at + tall : at + 2 * tall]
 
     wide = 2 * tall
 
-    def pixel_copy(which, step):
-        source = lax.rem(my_source + step, sources)
+    def pixel_copy(which, to, origin):
+        source = to[1] * 2 + to[2]
         return pltpu.make_async_remote_copy(
             src_ref=pixel_ref.at[which, source],
             dst_ref=landed_ref.at[which, my_source],
-            send_sem=pixel_send.at[which, step],
-            recv_sem=pixel_recv.at[which, step],
+            send_sem=pixel_send.at[which, source],
+            recv_sem=pixel_recv.at[which, origin],
             device_id=(my_owner, source),
             device_id_type=mesh_ids,
         )
 
+    def halves(value, axis):
+        high = value.astype(jnp.bfloat16)
+        low = (value - high.astype(jnp.float32)).astype(jnp.bfloat16)
+        return jnp.concatenate([high, low, high], axis=axis)
+
     def transform(which, real_part, imag_part):
-        spectrum = jnp.concatenate([real_part, imag_part], axis=0)
-        first = jnp.dot(
-            first_ref[...], spectrum, precision=highest, preferred_element_type=jnp.float32
-        )
+        spectrum = halves(jnp.concatenate([real_part, imag_part], axis=0), 0)
+        first = jnp.dot(first_ref[...], spectrum, preferred_element_type=jnp.float32)
         real, imag = first[:wide], first[wide:]
         twisted = jnp.concatenate(
             [
@@ -554,13 +548,13 @@
             axis=1,
         )
         both = lax.dot_general(
-            last_ref[...], twisted, NT, precision=highest, preferred_element_type=jnp.float32
+            last_ref[...], halves(twisted, 1), NT, preferred_element_type=jnp.float32
         )
         pixels = jnp.concatenate([both[:wide], both[wide:]], axis=1)
         for e in range(sources):
             pixel_ref[which, e] = pixels[e * 8 : e * 8 + 8]
-        for step in range(1, sources):
-            pixel_copy(which, step).start()
+        for device in same_owner:
+            pixel_copy(which, device, my_source).start()
         landed_ref[which, my_source] = pixel_ref[which, my_source]
 
     shifted = cycle_ref[lax.rem(my_owner, cycle_ref.shape[0])] % 2 == 1
@@ -570,25 +564,30 @@
 
     placed = place_spin(0)
     placed = placed + place_spin(1)
-    real, imag = joined(placed, 0), joined(placed, 3 * tall)
+    real, imag = joined(placed, 0), joined(placed, 2 * tall)
     transform(0, real * cosine - imag * sine, real * sine + imag * cosine)
 
+    placed = None
     for near in range(owners):
         ordered, pieces = received(2, near)
         for k in range(8):
             at = ((k // 4) * owners + near) * 4 + k % 4
             place(ordered[k : k + 1, :], pieces, k, 0, at)
-    placed = lax.dot_general(
-        left_ref[0 : 3 * tall, :], right_ref[...], NT, preferred_element_type=jnp.float32
-    )
+        for ab in range(2):
+            span = pl.ds((ab * owners + near) * 4 * LANES, 4 * LANES)
+            term = lax.dot_general(
+                left_ref[0 : 2 * tall, span], right_ref[:, span], NT, preferred_element_type=jnp.float32
+            )
+            placed = term if placed is None else placed + term
     value = joined(placed, 0)
     is_real = my_side == 0
     transform(1, value * jnp.where(is_real, cosine, -sine), value * jnp.where(is_real, sine, cosine))
     for piece in range(3):
-        fold(piece).wait_send()
+        for owner, line, side in others:
+            exchange(piece, (owner, line, side), (owner, side, line)).wait_send()
     for which in range(2):
-        for step in range(1, sources):
-            pixel_copy(which, step).wait()
+        for device in same_owner:
+            pixel_copy(which, device, device[1] * 2 + device[2]).wait()
     for c in range(4):
         out_ref[c] = landed_ref[1, 2 * c] + landed_ref[1, 2 * c + 1]
         out_ref[4 + c] = landed_ref[0, 2 * c]
@@ -610,7 +609,15 @@
     ids = np.concatenate([np.arange(0, LANES, 2), np.arange(1, LANES, 2)])
     angle = (ids[:, None] * np.arange(LANES)[None, :] % LANES) * (2 * np.pi / LANES)
     last = np.concatenate([np.cos(angle), -np.sin(angle)], axis=1)
-    return [jnp.asarray(t, jnp.float32) for t in (phase, first, twist, last)]
+
+    def halved(table):
+        high = table.astype(jnp.bfloat16)
+        low = (table - high.astype(np.float64)).astype(jnp.bfloat16)
+        return jnp.asarray(np.concatenate([high, high, low], axis=1))
+
+    return [
+        jnp.asarray(phase, jnp.float32), halved(first), jnp.asarray(twist, jnp.float32), halved(last)
+    ]
 
 
 def packed_body(legendre, harmonics, slot_orders, cycle_index):
@@ -653,20 +660,16 @@
             pltpu.VMEM((2, quads * 8, LANES), jnp.float32),
             pltpu.VMEM((quads * 4, LANES), jnp.float32),
             pltpu.VMEM((3, owners, 2, lines, 8, LANES), jnp.float32),
-            pltpu.VMEM((3, owners, lines, 8, LANES), jnp.float32),
-            pltpu.VMEM((3, owners, lines, 8, LANES), jnp.float32),
-            pltpu.VMEM((3, owners, lines, 8, LANES), jnp.float32),
-            pltpu.VMEM((6 * tall, width), jnp.bfloat16),
+            pltpu.VMEM((3, owners, 2, lines, 8, LANES), jnp.float32),
+            pltpu.VMEM((4 * tall, width), jnp.bfloat16),
             pltpu.VMEM((LANES, width), jnp.bfloat16),
             pltpu.VMEM((2, sources, 8, LANES), jnp.float32),
             pltpu.VMEM((2, sources, 8, LANES), jnp.float32),
             dma((7,)),
             dma((quads // SUB, 12)),
             dma((quads // 2 // SUB, 24)),
-            dma((3,)),
-            dma((3,)),
-            dma((3, owners * lines)),
-            dma((3, owners * lines)),
+            dma((3, owners, 2, lines)),
+            dma((3, owners, 2, lines)),
             dma((2, sources)),
             dma((2, sources)),
         ],

time: 27.9 us -> 26.7 us (0.957)
  Pallas kernels: 27.1 us -> 25.8 us
    pallas_call x1, Pallas kernels: 27.1 us -> 25.8 us  [packed_body(): pl.pallas_call(functools.partial(fused_kernel, width, slots, columns), in...]
where the time goes in v2:
time: 26.7 us; the launch traced here: 26.5 us
  Pallas kernels  25.8 us (97%)
  local copies, waits for them, and re-layouts  0.64 us (2%)
    pallas_call x1, Pallas kernels, packed_body(): pl.pallas_call(functools.partial(fused_kernel, width, slots, columns), in...  25.8 us
    reshape x1, local copies, waits for them, and re-layouts, packed_body(): return maps.reshape(1, 3, 4, 8 * LANES)  0.64 us

profile of v2, /device:TPU:0, one launch (start us, length us, event | category | flops | bytes accessed | tf_op | source)
XLA Modules:
  0.0 26.5 jit_solution(7675871302504295311)
XLA Ops:
  0.0 25.8 %shard_map.82 = f32[12,8,128]{2,1,0:T(8,128)S(1)} custom-call(s32[2]{0:T(128)} %cycle_hbm.1, s32[2048]{0:T(1024)} %orders_hbm.1, s32[4,4,128]{2,1,0:T(4,128)} %bitcast.13, bf16[3,4,128,2,4,128]{5,4,3,2,1,0:T(4,128)(2,1)} %bitcast.12, bf16[4,128,6,2,8,128]{5,4,3,2,1,0:T(8,128)(2,1)} %bitcast.11, f32[3,32,128]{2,1,0:T(8,128)} %constant.8.clone.phase_hbm, ...), custom_call_target="tpu_custom_call" | custom-call | tf_op jit(solution)/shard_map/pallas_call | solution.py:647
  25.8 0.6 %reshape.23 = f32[1,3,4,1024]{3,2,1,0:T(4,128)} reshape(f32[12,8,128]{2,1,0:T(8,128)S(1)} %shard_map.82) | data formatting | bytes 98304 | tf_op jit(solution)/shard_map/reshape | solution.py:680

commit v3 on v2

--- a/solution.py
+++ b/solution.py
@@ -573,12 +573,13 @@
         for k in range(8):
             at = ((k // 4) * owners + near) * 4 + k % 4
             place(ordered[k : k + 1, :], pieces, k, 0, at)
-        for ab in range(2):
-            span = pl.ds((ab * owners + near) * 4 * LANES, 4 * LANES)
-            term = lax.dot_general(
-                left_ref[0 : 2 * tall, span], right_ref[:, span], NT, preferred_element_type=jnp.float32
-            )
-            placed = term if placed is None else placed + term
+        if near % 2:
+            for ab in range(2):
+                span = pl.ds((ab * owners + near - 1) * 4 * LANES, 8 * LANES)
+                term = lax.dot_general(
+                    left_ref[0 : 2 * tall, span], right_ref[:, span], NT, preferred_element_type=jnp.float32
+                )
+                placed = term if placed is None else placed + term
     value = joined(placed, 0)
     is_real = my_side == 0
     transform(1, value * jnp.where(is_real, cosine, -sine), value * jnp.where(is_real, sine, cosine))

time: 26.7 us -> 26.6 us (level)
  no operation moved by 1% of the time
where the time goes in v3:
time: 26.6 us; the launch traced here: 26.4 us
  Pallas kernels  25.7 us (97%)
  local copies, waits for them, and re-layouts  0.64 us (2%)
    pallas_call x1, Pallas kernels, packed_body(): pl.pallas_call(functools.partial(fused_kernel, width, slots, columns), in...  25.7 us
    reshape x1, local copies, waits for them, and re-layouts, packed_body(): return maps.reshape(1, 3, 4, 8 * LANES)  0.64 us

profile of v3, /device:TPU:0, one launch (start us, length us, event | category | flops | bytes accessed | tf_op | source)
XLA Modules:
  0.0 26.4 jit_solution(9674170408344095115)
XLA Ops:
  0.0 25.7 %shard_map.82 = f32[12,8,128]{2,1,0:T(8,128)S(1)} custom-call(s32[2]{0:T(128)} %cycle_hbm.1, s32[2048]{0:T(1024)} %orders_hbm.1, s32[4,4,128]{2,1,0:T(4,128)} %bitcast.13, bf16[3,4,128,2,4,128]{5,4,3,2,1,0:T(4,128)(2,1)} %bitcast.12, bf16[4,128,6,2,8,128]{5,4,3,2,1,0:T(8,128)(2,1)} %bitcast.11, f32[3,32,128]{2,1,0:T(8,128)} %constant.8.clone.phase_hbm, ...), custom_call_target="tpu_custom_call" | custom-call | tf_op jit(solution)/shard_map/pallas_call | solution.py:648
  25.7 0.6 %reshape.23 = f32[1,3,4,1024]{3,2,1,0:T(4,128)} reshape(f32[12,8,128]{2,1,0:T(8,128)S(1)} %shard_map.82) | data formatting | bytes 98304 | tf_op jit(solution)/shard_map/reshape | solution.py:681
